TPU v7x, 32 devices: a whole 2x2x4 slice. The times are simulated.
32 devices in a mesh: seq: 8 (over y, x, core), tp: 4 (over z).
Axes of the slice: x: 2, y: 2, z: 4, core: 2. Of those that a mesh axis runs over, the one named last changes fastest.
Arguments:
- hidden_in: bfloat16 [2, 4096, 2560], P(None, 'seq'), may hold values from -6 to 6
- gate_proj: bfloat16 [2560, 5120], P(None, 'tp'), may hold values from -0.125 to 0.125
- value_proj: bfloat16 [2560, 5120], P(None, 'tp'), may hold values from -0.125 to 0.125
- bc_proj: bfloat16 [2560, 256], P(None, 'tp'), may hold values from -0.125 to 0.125
- step_proj: bfloat16 [2560, 80], P(None, 'tp'), may hold values from -0.125 to 0.125
- value_conv: float32 [4, 5120], P(None, 'tp'), may hold values from -3 to 3
- bc_conv: float32 [4, 256], replicated, may hold values from -3 to 3
- step_bias: float32 [80], P('tp'), may hold values from -1.5 to 0
- log_rate: float32 [80], P('tp'), as said below
- norm_gain: float32 [5120], P('tp'), may hold values from 0.25 to 1.75
Outputs:
- mixer_out: bfloat16 [2, 4096, 5120], P(None, 'seq', 'tp')
Inputs may be any that keep to these rules, and one draw needn't show every extreme that they name: log_rate lies between -1.5 - ln(4096) and 1.0 - ln(4096).
All inputs are finite; a program needn't handle non-finite values.
Results may differ from a plain program's by a relative error of at most 0.0095.
Values may be sent and summed in bfloat16 or wider, within the bound.
A program may use at most 128 MiB of HBM per device.

v0:
```python
import jax
import jax.numpy as jnp
from jax import lax
from jax.sharding import PartitionSpec as P

DI = 5120
HEAD_DIM = 64
STATE = 128
CONV = 4
BLOCK = 64


epsilon = 1e-05


def passed_along(block, axis, distance):
    devices = range(lax.axis_size(axis))
    route = [(i - distance, i) for i in devices if i - distance in devices]
    return lax.ppermute(block, axis, route)


def entering(part, axis, combine, identity, reverse):
    count = lax.axis_size(axis)
    place = lax.axis_index(axis)
    ahead = count - 1 - place if reverse else place
    gathered = jax.tree.map(lambda a: lax.all_gather(a, axis), part)
    state = jax.tree.map(lambda a, e: jnp.zeros_like(a) + jnp.asarray(e, a.dtype), part, identity)

    def one(step, state):
        source = count - 1 - step if reverse else step
        return combine(
            state, jax.tree.map(lambda a: lax.dynamic_index_in_dim(a, source, 0, False), gathered)
        )

    return lax.fori_loop(0, ahead, one, state)


def conv_silu(padded, kernel, length):
    running = jnp.zeros((padded.shape[0], length, padded.shape[2]), jnp.float32)
    for tap_index in range(kernel.shape[0]):
        running = running + kernel[tap_index] * padded[:, tap_index : tap_index + length, :]
    return jax.nn.silu(running)


def block_step(carried, inputs):
    values, log_decay, step_sizes, b_rows, c_rows = inputs
    length = log_decay.shape[1]
    cumulative = jnp.cumsum(log_decay, axis=1)
    log_gap = cumulative[:, :, None, :] - cumulative[:, None, :, :]
    causal = jnp.arange(length)[:, None] >= jnp.arange(length)[None, :]
    weights_in = jnp.exp(jnp.where(causal[None, :, :, None], log_gap, -jnp.inf))
    scores = jnp.einsum("bin,bjn->bij", c_rows, b_rows, precision=lax.Precision.HIGHEST)
    mixing = scores[:, :, :, None] * weights_in * step_sizes[:, None, :, :]
    within = jnp.einsum("bijh,bjhp->bihp", mixing, values, precision=lax.Precision.HIGHEST)
    earlier = jnp.einsum("bin,bhpn->bihp", c_rows, carried, precision=lax.Precision.HIGHEST)
    earlier = earlier * jnp.exp(cumulative)[..., None]
    remain = jnp.exp(cumulative[:, -1:, :] - cumulative) * step_sizes
    added_state = jnp.einsum(
        "bjh,bjhp,bjn->bhpn", remain, values, b_rows, precision=lax.Precision.HIGHEST
    )
    updated = jnp.exp(cumulative[:, -1, :])[:, :, None, None] * carried + added_state
    return (updated, within + earlier)


def to_blocks(series, batch_size, blocks):
    return jnp.moveaxis(series.reshape((batch_size, blocks, BLOCK) + series.shape[2:]), 1, 0)


def combine(earlier, latter):
    return (earlier[0] * latter[0], latter[0][:, :, None, None] * earlier[1] + latter[1])


def per_device(
    hidden_in,
    gate_proj,
    value_proj,
    bc_proj,
    step_proj,
    value_conv,
    bc_conv,
    step_bias,
    log_rate,
    norm_gain,
):
    batch_size, length, model_width = hidden_in.shape
    heads_here = step_proj.shape[1]
    inner_here = value_proj.shape[1]
    flat_rows = hidden_in.reshape(-1, model_width)
    gate_pre = jnp.dot(flat_rows, gate_proj, preferred_element_type=jnp.float32).astype(
        jnp.bfloat16
    )
    value_pre = jnp.dot(flat_rows, value_proj, preferred_element_type=jnp.float32).astype(
        jnp.bfloat16
    )
    step_pre = jnp.dot(flat_rows, step_proj, preferred_element_type=jnp.float32)
    bc_part = jnp.dot(flat_rows, bc_proj, preferred_element_type=jnp.float32).astype(jnp.bfloat16)
    bc_pre = lax.all_gather(bc_part, "tp", axis=1, tiled=True)
    joined = jnp.concatenate([value_pre, bc_pre], axis=1).reshape(batch_size, length, -1)
    tail_rows = joined[:, length - (CONV - 1) :, :]
    before = passed_along(tail_rows, "seq", 1)
    padded = jnp.concatenate([before, joined], axis=1).astype(jnp.float32)
    kernel = jnp.concatenate([value_conv, bc_conv], axis=1)
    mixed_in = conv_silu(padded, kernel, length)
    values = mixed_in[..., :inner_here].reshape(batch_size, length, heads_here, HEAD_DIM)
    b_rows = mixed_in[..., inner_here : inner_here + STATE]
    c_rows = mixed_in[..., inner_here + STATE :]
    step_sizes = jax.nn.softplus(step_pre.reshape(batch_size, length, heads_here) + step_bias)
    log_decay = -step_sizes * jnp.exp(log_rate)
    blocks = length // BLOCK
    initial = jnp.zeros((batch_size, heads_here, HEAD_DIM, STATE), jnp.float32)
    local_state, outputs = lax.scan(
        block_step,
        initial,
        (
            to_blocks(values, batch_size, blocks),
            to_blocks(log_decay, batch_size, blocks),
            to_blocks(step_sizes, batch_size, blocks),
            to_blocks(b_rows, batch_size, blocks),
            to_blocks(c_rows, batch_size, blocks),
        ),
    )
    within = jnp.moveaxis(outputs, 0, 1).reshape(batch_size, length, heads_here, HEAD_DIM)
    cumulative = jnp.cumsum(log_decay, axis=1)
    decays = jnp.exp(cumulative[:, -1, :])
    arrived = entering(
        (decays, local_state),
        "seq",
        combine,
        (jnp.ones_like(decays), jnp.zeros_like(local_state)),
        False,
    )[1]
    correction = jnp.einsum("btn,bhpn->bthp", c_rows, arrived, precision=lax.Precision.HIGHEST)
    correction = correction * jnp.exp(cumulative)[..., None]
    mixed_out = (within + correction).reshape(batch_size, length, inner_here)
    gated_out = mixed_out * jax.nn.silu(
        gate_pre.reshape(batch_size, length, inner_here).astype(jnp.float32)
    )
    squares = jnp.sum(gated_out * gated_out, axis=-1, keepdims=True)
    whole_sq = lax.psum(squares, "tp")
    return (gated_out * lax.rsqrt(whole_sq / DI + epsilon) * norm_gain).astype(jnp.bfloat16)


def solution(mesh):
    return jax.shard_map(
        per_device,
        mesh=mesh,
        in_specs=(
            P(None, "seq", None),
            P(None, "tp"),
            P(None, "tp"),
            P(None, "tp"),
            P(None, "tp"),
            P(None, "tp"),
            P(),
            P("tp"),
            P("tp"),
            P("tp"),
        ),
        out_specs=P(None, "seq", "tp"),
        check_vma=False,
    )
```

profile of v0, /device:TPU:7, one launch (start us, length us, event | category | flops | bytes accessed | tf_op | source)
XLA Modules:
  0.0 333.9 jit_solution(10901012978745536384)
XLA Ops:
  6.5 10.9 %convolution_convert_fusion.1 = bf16[1024,1280]{1,0:T(8,128)(2,1)S(1)} fusion(bf16[1024,2560]{1,0:T(8,128)(2,1)} %bitcast.138, bf16[2560,1280]{1,0:T(8,128)(2,1)} %param.16), kind=kOutput, calls=%fused_computation.57 | convolution fusion | flops 6712197120 | bytes 14417920 | tf_op jit(solution)/shard_map/dot_general | solution.py:92
  19.2 15.1 %all_gather.13 = bf16[1024,256]{0,1:T(8,128)(2,1)} all-gather(bf16[1024,64]{0,1:T(8,128)(2,1)S(1)} %convolution_convert_fusion.2), channel_id=1, replica_groups=mesh['seq'=8,'tp'=4] {'tp'}, dimensions={1}, use_global_device_ids=true | all-gather | bytes 655360 | tf_op jit(solution)/shard_map/all_gather | solution.py:97
  46.0 3.7 %divide_multiply_fusion = f32[2,512,1536]{2,1,0:T(8,128)S(1)} fusion(f32[2,515,1536]{2,1,0:T(8,128)S(1)} %maximum_convert_fusion, f32[1536]{0:T(1024)S(1)} %get-tuple-element.147, f32[1536]{0:T(1024)S(1)} %get-tuple-element.148, f32[1536]{0:T(1024)S(1)} %get-tuple-element.149, f32[1536]{0:T(1024)S(1)} %get-tuple-element.146), kind=kLoop, calls=%fused_computation.51 | loop fusion | flops 17301504 | bytes 31481856 | tf_op jit(solution)/shard_map/jit(silu)/mul | solution.py:42
  55.2 6.0 %copy.85 = f32[2,512,1280]{1,2,0:T(8,128)} copy(f32[2,512,1280]{2,1,0:T(8,128)} %slice.75) | data formatting | bytes 10485760 | tf_op jit(solution)/shard_map/slice | solution.py:104
  61.2 8.6 %reshape_reshape.3 = f32[2,8,64,20,64]{2,1,4,3,0:T(8,128)} reshape(f32[2,512,1280]{1,2,0:T(8,128)} %copy.85) | data formatting | bytes 10485760 | tf_op jit(solution)/shard_map/reshape;reshape | solution.py:66
  70.7 141.7 %while.26 = (s32[]{:T(128)}, f32[2,20,64,128]{3,2,1,0:T(8,128)S(1)}, f32[8,2,64,20,64]{2,4,3,1,0:T(8,128)}, f32[8,2,64,20]{2,0,1,3:T(8,128)}, f32[8,2,64,20]{2,0...) while((s32[]{:T(128)}, ...), condition=%wide.region_2.3_spmd.clone, body=%wide.region_0.2_spmd.clone.sunk | while | flops 644356608 | bytes 10450500 | solution.py:111
  73.1 5.3 %constant_dynamic-slice_fusion.5 = f32[1,2,64,20,64]{2,0,4,3,1:T(1,128)S(1)} fusion(f32[8,2,64,20,64]{2,0,4,3,1:T(8,128)} %get-tuple-element.305, s32[]{:T(128)} %get-tuple-element.289), kind=kLoop, calls=%fused_computation.39.clone.1 | loop fusion | bytes 1310724 | tf_op jit(solution)/shard_map/while/body/jit(dynamic_index_in_dim)/dynamic_slice | solution.py:111
  82.2 3.6 %fusion.78 = f32[8,2,64,20,64]{2,4,3,1,0:T(8,128)} fusion(f32[8,2,64,20,64]{2,4,3,1,0:T(8,128)} %get-tuple-element.291, s32[]{:T(128)} %get-tuple-element.289, f32[2,64,20,64]{1,3,2,0:T(8,128)} %convolution_bitcast_fusion.2, f32[2,20,64,128]{3,2,1,0:T(8,128)S(1)} %get-tuple-element.290, f32[2,64,20]{1,2,0:T(8,128)S(1)} %copy.130, pred[]{:T(512)S(6)} %compare.3, ...), kind=kOutput, calls=%fused_computation.5.clone.1 | convolution fusion | flops 252313600 | bytes 4023297 | tf_op jit(solution)/shard_map/while/body/eval_jaxpr/bin,bhpn->bihp/dot_general | solution.py:55
  90.8 5.3 %constant_dynamic-slice_fusion.5 = f32[1,2,64,20,64]{2,0,4,3,1:T(1,128)S(1)} fusion(f32[8,2,64,20,64]{2,0,4,3,1:T(8,128)} %get-tuple-element.305, s32[]{:T(128)} %get-tuple-element.289), kind=kLoop, calls=%fused_computation.39.clone.1 | loop fusion | bytes 1310724 | tf_op jit(solution)/shard_map/while/body/jit(dynamic_index_in_dim)/dynamic_slice | solution.py:111
  99.9 3.6 %fusion.78 = f32[8,2,64,20,64]{2,4,3,1,0:T(8,128)} fusion(f32[8,2,64,20,64]{2,4,3,1,0:T(8,128)} %get-tuple-element.291, s32[]{:T(128)} %get-tuple-element.289, f32[2,64,20,64]{1,3,2,0:T(8,128)} %convolution_bitcast_fusion.2, f32[2,20,64,128]{3,2,1,0:T(8,128)S(1)} %get-tuple-element.290, f32[2,64,20]{1,2,0:T(8,128)S(1)} %copy.130, pred[]{:T(512)S(6)} %compare.3, ...), kind=kOutput, calls=%fused_computation.5.clone.1 | convolution fusion | flops 252313600 | bytes 4023297 | tf_op jit(solution)/shard_map/while/body/eval_jaxpr/bin,bhpn->bihp/dot_general | solution.py:55
  108.6 5.3 %constant_dynamic-slice_fusion.5 = f32[1,2,64,20,64]{2,0,4,3,1:T(1,128)S(1)} fusion(f32[8,2,64,20,64]{2,0,4,3,1:T(8,128)} %get-tuple-element.305, s32[]{:T(128)} %get-tuple-element.289), kind=kLoop, calls=%fused_computation.39.clone.1 | loop fusion | bytes 1310724 | tf_op jit(solution)/shard_map/while/body/jit(dynamic_index_in_dim)/dynamic_slice | solution.py:111
  117.6 3.6 %fusion.78 = f32[8,2,64,20,64]{2,4,3,1,0:T(8,128)} fusion(f32[8,2,64,20,64]{2,4,3,1,0:T(8,128)} %get-tuple-element.291, s32[]{:T(128)} %get-tuple-element.289, f32[2,64,20,64]{1,3,2,0:T(8,128)} %convolution_bitcast_fusion.2, f32[2,20,64,128]{3,2,1,0:T(8,128)S(1)} %get-tuple-element.290, f32[2,64,20]{1,2,0:T(8,128)S(1)} %copy.130, pred[]{:T(512)S(6)} %compare.3, ...), kind=kOutput, calls=%fused_computation.5.clone.1 | convolution fusion | flops 252313600 | bytes 4023297 | tf_op jit(solution)/shard_map/while/body/eval_jaxpr/bin,bhpn->bihp/dot_general | solution.py:55
  126.3 5.3 %constant_dynamic-slice_fusion.5 = f32[1,2,64,20,64]{2,0,4,3,1:T(1,128)S(1)} fusion(f32[8,2,64,20,64]{2,0,4,3,1:T(8,128)} %get-tuple-element.305, s32[]{:T(128)} %get-tuple-element.289), kind=kLoop, calls=%fused_computation.39.clone.1 | loop fusion | bytes 1310724 | tf_op jit(solution)/shard_map/while/body/jit(dynamic_index_in_dim)/dynamic_slice | solution.py:111
  144.0 5.3 %constant_dynamic-slice_fusion.5 = f32[1,2,64,20,64]{2,0,4,3,1:T(1,128)S(1)} fusion(f32[8,2,64,20,64]{2,0,4,3,1:T(8,128)} %get-tuple-element.305, s32[]{:T(128)} %get-tuple-element.289), kind=kLoop, calls=%fused_computation.39.clone.1 | loop fusion | bytes 1310724 | tf_op jit(solution)/shard_map/while/body/jit(dynamic_index_in_dim)/dynamic_slice | solution.py:111
  153.0 3.6 %fusion.78 = f32[8,2,64,20,64]{2,4,3,1,0:T(8,128)} fusion(f32[8,2,64,20,64]{2,4,3,1,0:T(8,128)} %get-tuple-element.291, s32[]{:T(128)} %get-tuple-element.289, f32[2,64,20,64]{1,3,2,0:T(8,128)} %convolution_bitcast_fusion.2, f32[2,20,64,128]{3,2,1,0:T(8,128)S(1)} %get-tuple-element.290, f32[2,64,20]{1,2,0:T(8,128)S(1)} %copy.130, pred[]{:T(512)S(6)} %compare.3, ...), kind=kOutput, calls=%fused_computation.5.clone.1 | convolution fusion | flops 252313600 | bytes 4023297 | tf_op jit(solution)/shard_map/while/body/eval_jaxpr/bin,bhpn->bihp/dot_general | solution.py:55
  161.6 5.3 %constant_dynamic-slice_fusion.5 = f32[1,2,64,20,64]{2,0,4,3,1:T(1,128)S(1)} fusion(f32[8,2,64,20,64]{2,0,4,3,1:T(8,128)} %get-tuple-element.305, s32[]{:T(128)} %get-tuple-element.289), kind=kLoop, calls=%fused_computation.39.clone.1 | loop fusion | bytes 1310724 | tf_op jit(solution)/shard_map/while/body/jit(dynamic_index_in_dim)/dynamic_slice | solution.py:111
  170.7 3.6 %fusion.78 = f32[8,2,64,20,64]{2,4,3,1,0:T(8,128)} fusion(f32[8,2,64,20,64]{2,4,3,1,0:T(8,128)} %get-tuple-element.291, s32[]{:T(128)} %get-tuple-element.289, f32[2,64,20,64]{1,3,2,0:T(8,128)} %convolution_bitcast_fusion.2, f32[2,20,64,128]{3,2,1,0:T(8,128)S(1)} %get-tuple-element.290, f32[2,64,20]{1,2,0:T(8,128)S(1)} %copy.130, pred[]{:T(512)S(6)} %compare.3, ...), kind=kOutput, calls=%fused_computation.5.clone.1 | convolution fusion | flops 252313600 | bytes 4023297 | tf_op jit(solution)/shard_map/while/body/eval_jaxpr/bin,bhpn->bihp/dot_general | solution.py:55
  179.4 5.3 %constant_dynamic-slice_fusion.5 = f32[1,2,64,20,64]{2,0,4,3,1:T(1,128)S(1)} fusion(f32[8,2,64,20,64]{2,0,4,3,1:T(8,128)} %get-tuple-element.305, s32[]{:T(128)} %get-tuple-element.289), kind=kLoop, calls=%fused_computation.39.clone.1 | loop fusion | bytes 1310724 | tf_op jit(solution)/shard_map/while/body/jit(dynamic_index_in_dim)/dynamic_slice | solution.py:111
  188.4 3.6 %fusion.78 = f32[8,2,64,20,64]{2,4,3,1,0:T(8,128)} fusion(f32[8,2,64,20,64]{2,4,3,1,0:T(8,128)} %get-tuple-element.291, s32[]{:T(128)} %get-tuple-element.289, f32[2,64,20,64]{1,3,2,0:T(8,128)} %convolution_bitcast_fusion.2, f32[2,20,64,128]{3,2,1,0:T(8,128)S(1)} %get-tuple-element.290, f32[2,64,20]{1,2,0:T(8,128)S(1)} %copy.130, pred[]{:T(512)S(6)} %compare.3, ...), kind=kOutput, calls=%fused_computation.5.clone.1 | convolution fusion | flops 252313600 | bytes 4023297 | tf_op jit(solution)/shard_map/while/body/eval_jaxpr/bin,bhpn->bihp/dot_general | solution.py:55
  197.1 5.3 %constant_dynamic-slice_fusion.5 = f32[1,2,64,20,64]{2,0,4,3,1:T(1,128)S(1)} fusion(f32[8,2,64,20,64]{2,0,4,3,1:T(8,128)} %get-tuple-element.305, s32[]{:T(128)} %get-tuple-element.289), kind=kLoop, calls=%fused_computation.39.clone.1 | loop fusion | bytes 1310724 | tf_op jit(solution)/shard_map/while/body/jit(dynamic_index_in_dim)/dynamic_slice | solution.py:111
  206.2 3.6 %fusion.78 = f32[8,2,64,20,64]{2,4,3,1,0:T(8,128)} fusion(f32[8,2,64,20,64]{2,4,3,1,0:T(8,128)} %get-tuple-element.291, s32[]{:T(128)} %get-tuple-element.289, f32[2,64,20,64]{1,3,2,0:T(8,128)} %convolution_bitcast_fusion.2, f32[2,20,64,128]{3,2,1,0:T(8,128)S(1)} %get-tuple-element.290, f32[2,64,20]{1,2,0:T(8,128)S(1)} %copy.130, pred[]{:T(512)S(6)} %compare.3, ...), kind=kOutput, calls=%fused_computation.5.clone.1 | convolution fusion | flops 252313600 | bytes 4023297 | tf_op jit(solution)/shard_map/while/body/eval_jaxpr/bin,bhpn->bihp/dot_general | solution.py:55
  217.9 12.7 %fusion.36 = f32[1024,1280]{1,0:T(8,128)} fusion(bf16[1024,2560]{1,0:T(8,128)(2,1)} %bitcast.139, bf16[2560,1280]{1,0:T(8,128)(2,1)} %param.15), kind=kOutput, calls=%fused_computation.56 | convolution fusion | flops 6713507840 | bytes 17039360 | tf_op jit(solution)/shard_map/dot_general | solution.py:89
  230.7 6.0 %copy.99 = f32[1024,1280]{0,1:T(8,128)} copy(f32[1024,1280]{1,0:T(8,128)} %fusion.36) | data formatting | bytes 10485760 | tf_op jit(solution)/shard_map/convert_element_type | solution.py:136
  236.6 8.1 %reshape.101 = f32[2,512,20,64]{1,0,3,2:T(2,128)} reshape(f32[1024,1280]{0,1:T(8,128)} %copy.99) | data formatting | bytes 10485760 | tf_op jit(solution)/shard_map/convert_element_type | solution.py:136
  244.8 10.0 %all-gather = f32[16,1,20]{2,1,0:T(1,128)S(1)} all-gather(f32[2,1,20]{2,1,0:T(1,128)S(1)} %bitcast.155), channel_id=2, replica_groups=mesh['seq'=8,'tp'=4] {'seq'}, dimensions={0}, use_global_device_ids=true | all-gather | bytes 1440 | tf_op jit(solution)/shard_map/all_gather | solution.py:26
  254.8 17.8 %copy.91 = f32[2,8,64,20,64]{2,1,4,3,0:T(8,128)} copy(f32[2,8,64,20,64]{2,4,3,0,1:T(8,128)} %bitcast.144) | data formatting | bytes 10485760 | tf_op jit(solution)/shard_map/transpose | solution.py:122
  272.6 9.4 %reshape.96 = f32[2,512,20,64]{1,3,2,0:T(8,128)} reshape(f32[2,8,64,20,64]{2,1,4,3,0:T(8,128)} %copy.91) | data formatting | bytes 10485760 | tf_op jit(solution)/shard_map/reshape | solution.py:122
  282.2 11.5 %while.25 = (s32[]{:T(128)}, f32[2,20,64,128]{3,2,1,0:T(8,128)S(1)}, s32[]{:T(128)}, f32[8,2,20]{2,1,0:T(2,128)S(1)}, f32[8,2,20,64,128]{4,3,2,1,0:T(8,128)}, /*index=5*/s32[]{:T(128)}, s32[]{:T(128)}, s32[]{:T(128)}) while((s32[]{:T(128)}, f32[2,20,64,128]{3,2,1,0:T(8,128)S(1)}, s32[]{:T(128)}, f32[8,2,20]{2,1,0:T(2,128)S(1)}, ...), condition=%wide.region_6.7_spmd, body=%wide.region_5.6_spmd.sunk | while | flops 655365 | bytes 3932767 | solution.py:35
  293.7 10.4 %multiply_reduce_fusion = (f32[2,512]{1,0:T(2,128)S(1)}, f32[2,512,20,64]{1,3,2,0:T(8,128)}) fusion(f32[2,512,20,64]{1,0,3,2:T(2,128)} %reshape.101, f32[2,512,20,64]{1,3,2,0:T(8,128)} %reshape.96, f32[2,512,20]{1,2,0:T(8,128)S(1)} %copy.97, f32[2,20,64,128]{3,2,1,0:T(8,128)S(1)} %get-tuple-element.94, f32[2,512,1536]{2,1,0:T(8,128)} %copy-done.3), kind=kOutput, calls=%fused_computation.53 | convolution fusion | flops 2025061376 | bytes 17649664 | tf_op jit(solution)/shard_map/btn,bhpn->bthp/dot_general | solution.py:132
  304.1 5.9 %copy.98 = f32[2,512,1280]{2,1,0:T(8,128)} copy(f32[2,512,1280]{1,2,0:T(8,128)} %bitcast.146) | data formatting | bytes 10485760 | tf_op jit(solution)/shard_map/reshape | solution.py:134
  310.0 10.7 %psum.7 = f32[2,512,1]{1,0,2:T(2,128)S(1)} all-reduce(f32[2,512,1]{1,0,2:T(2,128)S(1)} %bitcast.156), channel_id=1, replica_groups=mesh['seq'=8,'tp'=4] {'tp'}, use_global_device_ids=true, to_apply=%region_8.9 | all-reduce | flops 1024 | bytes 8192 | tf_op jit(solution)/shard_map/psum | solution.py:139
  320.8 6.1 %multiply_convert_fusion = bf16[2,512,1280]{2,1,0:T(8,128)(2,1)} fusion(f32[2,512,1280]{2,1,0:T(8,128)} %copy.98, f32[2,512,1280]{2,1,0:T(8,128)} %bitcast.141, f32[1280]{0:T(1024)S(1)} %copy-done.9, f32[2,512]{1,0:T(2,128)S(1)} %rsqrt_bitcast_fusion), kind=kLoop, calls=%fused_computation.52 | loop fusion | flops 10485760 | bytes 13116416 | tf_op jit(solution)/shard_map/convert_element_type | solution.py:140
  (199 shorter events, 110.0 us)
Async XLA Ops:
  6.5 10.9 %copy-start = (bf16[2560,64]{0,1:T(8,128)(2,1)S(1)}, bf16[2560,64]{0,1:T(8,128)(2,1)}, u32[]{:S(2)}) copy-start(bf16[2560,64]{0,1:T(8,128)(2,1)} %param.17) | copy-start | bytes 983044
  6.5 275.5 %all-gather.4.cloned.1.call-start = ((), (), s32[]{:S(2)}) async-start(), calls=%async_computation | async-start | bytes 11796480 | tf_op jit(solution)/shard_map/all_gather | solution.py:26
  6.5 10.9 %copy-start.4 = (bf16[2,512,2560]{2,1,0:T(8,128)(2,1)S(1)}, bf16[2,512,2560]{2,1,0:T(8,128)(2,1)}, u32[]{:S(2)}) copy-start(bf16[2,512,2560]{2,1,0:T(8,128)(2,1)} %param.14) | copy-start | bytes 15728644
  19.2 18.5 %copy-start.8 = (f32[4,1280]{1,0:T(4,128)S(1)}, f32[4,1280]{1,0:T(4,128)}, u32[]{:S(2)}) copy-start(f32[4,1280]{1,0:T(4,128)} %param.19) | copy-start | bytes 61444
  19.2 18.5 %copy-start.12 = (f32[20]{0:T(128)S(1)}, f32[20]{0:T(128)}, u32[]{:S(2)}) copy-start(f32[20]{0:T(128)} %param.22) | copy-start | bytes 244
  19.2 18.5 %copy-start.10 = (f32[4,256]{1,0:T(4,128)S(1)}, f32[4,256]{1,0:T(4,128)}, u32[]{:S(2)}) copy-start(f32[4,256]{1,0:T(4,128)} %param.20) | copy-start | bytes 12292
  19.2 18.5 %copy-start.7 = (bf16[2560,20]{0,1:T(8,128)(2,1)S(1)}, bf16[2560,20]{0,1:T(8,128)(2,1)}, u32[]{:S(2)}) copy-start(bf16[2560,20]{0,1:T(8,128)(2,1)} %param.18) | copy-start | bytes 307204
  19.2 18.5 %copy-start.11 = (f32[20]{0:T(128)S(1)}, f32[20]{0:T(128)}, u32[]{:S(2)}) copy-start(f32[20]{0:T(128)} %param.21) | copy-start | bytes 244
  35.6 3.6 %copy-start.5 = (bf16[2,512,2560]{2,1,0:T(8,128)(2,1)S(1)}, bf16[2,512,2560]{2,1,0:T(8,128)(2,1)}, u32[]{:S(2)}) copy-start(bf16[2,512,2560]{2,1,0:T(8,128)(2,1)} %param.14) | copy-start | bytes 15728644
  35.8 5.5 %copy-start.6 = (bf16[1024,1536]{1,0:T(8,128)(2,1)}, bf16[1024,1536]{1,0:T(8,128)(2,1)S(1)}, u32[]{:S(2)}) copy-start(bf16[1024,1536]{1,0:T(8,128)(2,1)S(1)} %pad_maximum_fusion) | copy-start | bytes 9437188
  35.9 7.3 %collective-permute-start = (bf16[2,3,1536]{2,1,0:T(4,128)(2,1)S(1)}, bf16[2,3,1536]{2,1,0:T(4,128)(2,1)S(1)}, u32[]{:S(2)}, u32[]{:S(2)}) collective-permute-start(bf16[2,3,1536]{2,1,0:T(4,128)(2,1)S(1)} %slice.67), channel_id=1, source_target_pairs={{0,4},{4,8},{8,12},{12,16},{16,20},{20,24},{24,28},{1,5},{5,9},{9,... | collective-permute-start | bytes 55304 | tf_op jit(solution)/shard_map/ppermute | solution.py:19
  49.7 2.7 copy-start.3
  212.4 1.1 copy-start.2
  304.1 16.7 %copy-start.9 = (f32[1280]{0:T(1024)S(1)}, f32[1280]{0:T(1024)}, u32[]{:S(2)}) copy-start(f32[1280]{0:T(1024)} %param.23) | copy-start | bytes 15364
  320.8 6.1 %copy-start.1 = (bf16[2560,64]{0,1:T(8,128)(2,1)S(1)}, bf16[2560,64]{0,1:T(8,128)(2,1)}, u32[]{:S(2)}) copy-start(bf16[2560,64]{0,1:T(8,128)(2,1)} %param.17) | copy-start | bytes 983044
Sparse Core Ops, SparseCore 0:
  213.6 65.9 all-gather.3
where the time goes:
time: 340 us; the launch traced here: 334 us
  local copies, waits for them, and re-layouts  129 us (38%)
  matrix products  124 us (36%)
  blocking collectives  35.8 us (11%)
  other arithmetic  28.4 us (8%)
  between operations  13.9 us (4%)
    dynamic_slice x32, local copies, waits for them, and re-layouts, per_device(): lax.scan(block_step, initial, (to_blocks(values, batch_size, blocks), to_...  52.1 us
    dot_general x8, matrix products, block_step(): jnp.einsum('bin,bhpn->bihp', c_rows, carried, precision=lax.Precision.HIG...  28.8 us
    dot_general x8, matrix products, block_step(): jnp.einsum('bijh,bjhp->bihp', mixing, values, precision=lax.Precision.HIG...  28.4 us
    dot_general x8, matrix products, block_step(): jnp.einsum('bjh,bjhp,bjn->bhpn', remain, values, b_rows, precision=lax.Pr...  20 us
    transpose x1, local copies, waits for them, and re-layouts, per_device(): jnp.moveaxis(outputs, 0, 1)  17.8 us
    all_gather x1, blocking collectives, per_device(): bc_pre = lax.all_gather(bc_part, 'tp', axis=1, tiled=True)  15.1 us
    convert_element_type x2, local copies, waits for them, and re-layouts, per_device(): gate_pre.reshape(batch_size, length, inner_here).astype(jnp.float32)  14.1 us
    dot_general x1, matrix products, per_device(): jnp.dot(flat_rows, gate_proj, preferred_element_type=jnp.float32)  12.7 us
  transfers between devices with their start and end apart: 2, of which 0 were waited for; matrix products, arithmetic and copies ran while one was open for 19% of the time, Pallas kernels for 0%

commit v1 on v0

v1 whole, which is shorter than its diff:
```python
import jax
import jax.numpy as jnp
from jax import lax
from jax.experimental import pallas as pl
from jax.experimental.pallas import tpu as pltpu
from jax.sharding import PartitionSpec as P

DI = 5120
HEAD_DIM = 64
STATE = 128
CONV = 4
BLOCK = 64
PAD = 8

epsilon = 1e-05
F32 = jnp.float32
BF16 = jnp.bfloat16


def shifted(block, axis, distance):
    count = lax.axis_size(axis)
    route = [(i, i + distance) for i in range(count - distance)]
    return lax.ppermute(block, axis, route)


def silu(x):
    return x * (1.0 / (1.0 + jnp.exp(-x)))


def spread(x, expand):
    high = x.astype(BF16)
    low = (x - high.astype(F32)).astype(BF16)
    return jnp.dot(jnp.concatenate([high, low], axis=1), expand, preferred_element_type=F32)


def tile_of(width):
    return 256 if width % 256 == 0 else 128


def state_kernel(
    pre_ref, pre_halo_ref, bc_ref, bc_halo_ref, step_ref, kernel_ref, bc_kernel_ref,
    bias_ref, rate_ref, expand_ref,
    scaled_ref, bc_out_ref, fout_ref, em_ref, state_ref, decay_ref,
    window, bc_window, lows,
):
    length, width = pre_ref.shape[1], pre_ref.shape[2]
    tile = tile_of(width)
    window[0:PAD, :] = pre_halo_ref[0].astype(F32)
    bc_window[0:PAD, :] = bc_halo_ref[0].astype(F32)
    state_ref[...] = jnp.zeros_like(state_ref)
    heads = bias_ref.shape[1]
    rows = lax.broadcasted_iota(jnp.int32, (BLOCK, BLOCK), 0)
    cols = lax.broadcasted_iota(jnp.int32, (BLOCK, BLOCK), 1)
    triangle = jnp.where(rows >= cols, 1.0, 0.0).astype(F32)
    lows[...] = jnp.zeros_like(lows)

    @pl.loop(0, length // BLOCK)
    def _(index):
        at = pl.ds(pl.multiple_of(index * BLOCK, BLOCK), BLOCK)
        step_pre = step_ref[0, at, :] + bias_ref[...]
        steps = jnp.maximum(step_pre, 0.0) + jnp.log1p(jnp.exp(-jnp.abs(step_pre)))
        log_decay = -steps * jnp.exp(rate_ref[...])
        cumulative = jnp.dot(
            triangle, log_decay, precision=lax.Precision.HIGHEST, preferred_element_type=F32
        )
        last = cumulative[BLOCK - 1 : BLOCK, :]
        lows[0:1, :] += last
        mid = 0.5 * last
        fin = jnp.exp(mid - cumulative) * steps
        fout_ref[0, at, :] = jnp.exp(cumulative - mid)
        em = jnp.broadcast_to(jnp.exp(mid), (8, heads))
        em_ref[0, pl.ds(pl.multiple_of(index * 8, 8), 8), :] = em
        wide_fin = spread(fin, expand_ref[...])
        wide_em = spread(em, expand_ref[...])[0:1, :]

        bc_window[PAD:, :] = bc_ref[0, at, :].astype(F32)
        bc = bc_kernel_ref[0:1, :] * bc_window[5 : 5 + BLOCK, :]
        for k in range(1, CONV):
            bc = bc + bc_kernel_ref[k : k + 1, :] * bc_window[5 + k : 5 + k + BLOCK, :]
        bc = silu(bc).astype(BF16)
        bc_out_ref[0, at, :] = bc
        bc_window[0:PAD, :] = bc_window[BLOCK : BLOCK + PAD, :]
        b_rows = bc[:, :STATE]

        for start in range(0, width, tile):
            cut = slice(start, start + tile)
            window[PAD:, cut] = pre_ref[0, at, cut].astype(F32)
            x = kernel_ref[0:1, cut] * window[5 : 5 + BLOCK, cut]
            for k in range(1, CONV):
                x = x + kernel_ref[k : k + 1, cut] * window[5 + k : 5 + k + BLOCK, cut]
            scaled = (silu(x) * wide_fin[:, cut]).astype(BF16)
            window[0:PAD, cut] = window[BLOCK : BLOCK + PAD, cut]
            scaled_ref[0, at, cut] = scaled
            added = lax.dot_general(
                b_rows, scaled, (((0,), (0,)), ((), ())), preferred_element_type=F32
            )
            e = wide_em[:, cut]
            state_ref[0, :, cut] = e * (e * state_ref[0, :, cut] + added)

    decay_ref[0] = spread(jnp.exp(lows[...]), expand_ref[...])


def output_kernel(
    scaled_ref, bc_ref, fout_ref, em_ref, state_ref, gate_ref, expand_ref,
    gated_ref, squares_ref, held, right,
):
    length, width = scaled_ref.shape[1], scaled_ref.shape[2]
    tile = tile_of(width)
    held[...] = state_ref[0]
    rows = lax.broadcasted_iota(jnp.int32, (BLOCK, BLOCK), 0)
    cols = lax.broadcasted_iota(jnp.int32, (BLOCK, BLOCK), 1)

    @pl.loop(0, length // BLOCK)
    def _(index):
        at = pl.ds(pl.multiple_of(index * BLOCK, BLOCK), BLOCK)
        wide_fout = spread(fout_ref[0, at, :], expand_ref[...])
        em = em_ref[0, pl.ds(pl.multiple_of(index * 8, 8), 8), :]
        wide_em = spread(em, expand_ref[...])[0:1, :]
        b_rows = bc_ref[0, at, :STATE]
        c_rows = bc_ref[0, at, STATE:]
        scores = lax.dot_general(
            c_rows, b_rows, (((1,), (1,)), ((), ())), preferred_element_type=F32
        )
        mixing = jnp.where(rows >= cols, scores, 0.0).astype(BF16)
        left = jnp.concatenate([c_rows, mixing], axis=1)
        total = jnp.zeros((BLOCK, 128), F32)
        for start in range(0, width, tile):
            cut = slice(start, start + tile)
            scaled = scaled_ref[0, at, cut]
            e = wide_em[:, cut]
            entering = e * held[:, cut]
            right[:STATE, cut] = entering.astype(BF16)
            right[STATE:, cut] = scaled
            y = jnp.dot(left, right[:, cut], preferred_element_type=F32)
            added = lax.dot_general(
                b_rows, scaled, (((0,), (0,)), ((), ())), preferred_element_type=F32
            )
            held[:, cut] = e * (entering + added)
            gated = y * wide_fout[:, cut] * silu(gate_ref[0, at, cut].astype(F32))
            gated_ref[0, at, cut] = gated.astype(gated_ref.dtype)
            squared = gated * gated
            for piece in range(0, tile, 128):
                total = total + squared[:, piece : piece + 128]
        squares_ref[0, at, :] = jnp.sum(total, axis=1, keepdims=True)


def one_batch(shape):
    return pl.BlockSpec((1,) + tuple(shape[1:]), lambda b: (b,) + (0,) * (len(shape) - 1))


def whole(shape):
    return pl.BlockSpec(tuple(shape), lambda b: (0,) * len(shape))


def per_device(
    hidden_in, gate_proj, value_proj, bc_proj, step_proj,
    value_conv, bc_conv, step_bias, log_rate, norm_gain,
):
    batch, length, model_width = hidden_in.shape
    heads = step_proj.shape[1]
    width = value_proj.shape[1]
    narrow = bc_proj.shape[1]
    blocks = length // BLOCK
    flat = hidden_in.reshape(-1, model_width)
    halo_in = shifted(hidden_in[:, length - PAD :, :], "seq", 1)
    halo_flat = halo_in.reshape(-1, model_width)

    small = jnp.concatenate([bc_proj, step_proj], axis=1)
    small_pre = jnp.dot(flat, small, preferred_element_type=F32)
    step_pre = small_pre[:, narrow:].reshape(batch, length, heads)
    bc_part = small_pre[:, :narrow].astype(BF16)
    bc_halo = jnp.dot(halo_flat, bc_proj, preferred_element_type=F32).astype(BF16)
    bc_all = lax.all_gather(
        jnp.concatenate([bc_halo, bc_part], axis=0), "tp", axis=1, tiled=True
    )
    bc_halo = bc_all[: batch * PAD].reshape(batch, PAD, -1)
    bc_pre = bc_all[batch * PAD :].reshape(batch, length, -1)
    value_pre = jnp.dot(flat, value_proj, preferred_element_type=F32).astype(BF16)
    value_halo = jnp.dot(halo_flat, value_proj, preferred_element_type=F32).astype(BF16)
    value_pre = value_pre.reshape(batch, length, width)
    value_halo = value_halo.reshape(batch, PAD, width)

    lanes = lax.broadcasted_iota(jnp.int32, (2 * heads, width), 1) // HEAD_DIM
    owner = lax.broadcasted_iota(jnp.int32, (2 * heads, width), 0) % heads
    expand = (lanes == owner).astype(BF16)
    bias = step_bias.reshape(1, heads)
    rate = log_rate.reshape(1, heads)

    ins = (value_pre, value_halo, bc_pre, bc_halo, step_pre)
    fixed = (value_conv, bc_conv, bias, rate, expand)
    outs = (
        jax.ShapeDtypeStruct((batch, length, width), BF16),
        jax.ShapeDtypeStruct((batch, length, 2 * STATE), BF16),
        jax.ShapeDtypeStruct((batch, length, heads), F32),
        jax.ShapeDtypeStruct((batch, blocks * 8, heads), F32),
        jax.ShapeDtypeStruct((batch, STATE, width), F32),
        jax.ShapeDtypeStruct((batch, 8, width), F32),
    )
    scaled, bc, fout, em, local_state, decay = pl.pallas_call(
        state_kernel,
        grid=(batch,),
        out_shape=outs,
        in_specs=[one_batch(a.shape) for a in ins] + [whole(a.shape) for a in fixed],
        out_specs=[one_batch(a.shape) for a in outs],
        scratch_shapes=[
            pltpu.VMEM((BLOCK + PAD, width), F32),
            pltpu.VMEM((BLOCK + PAD, 2 * STATE), F32),
            pltpu.VMEM((8, heads), F32),
        ],
        compiler_params=pltpu.CompilerParams(vmem_limit_bytes=48 << 20),
        cost_estimate=pl.CostEstimate(
            flops=1 << 30, bytes_accessed=8 << 20, transcendentals=1 << 21
        ),
        name="state",
    )(*ins, *fixed)

    decay = decay[:, 0:1, :]
    count = lax.axis_size("seq")
    through, span = local_state, decay
    before, before_span = jnp.zeros_like(local_state), jnp.ones_like(decay)
    distance = 1
    while distance < count:
        got = shifted(through.astype(BF16), "seq", distance).astype(F32)
        before = before + before_span * got
        if 2 * distance < count:
            got_span = shifted(span, "seq", distance)
            through = through + span * got
            has = lax.axis_index("seq") >= distance
            got_span = jnp.where(has, got_span, 1.0)
            before_span = before_span * got_span
            span = span * got_span
        distance *= 2

    gate_pre = jnp.dot(flat, gate_proj, preferred_element_type=F32).astype(BF16)
    gate_pre = gate_pre.reshape(batch, length, width)
    ins = (scaled, bc, fout, em, before, gate_pre)
    outs = (
        jax.ShapeDtypeStruct((batch, length, width), BF16),
        jax.ShapeDtypeStruct((batch, length, 1), F32),
    )
    gated, squares = pl.pallas_call(
        output_kernel,
        grid=(batch,),
        out_shape=outs,
        in_specs=[one_batch(a.shape) for a in ins] + [whole(expand.shape)],
        out_specs=[one_batch(a.shape) for a in outs],
        scratch_shapes=[
            pltpu.VMEM((STATE, width), F32),
            pltpu.VMEM((STATE + BLOCK, width), BF16),
        ],
        compiler_params=pltpu.CompilerParams(vmem_limit_bytes=48 << 20),
        cost_estimate=pl.CostEstimate(
            flops=1 << 30, bytes_accessed=8 << 20, transcendentals=1 << 21
        ),
        name="outputs",
    )(*ins, expand)
    whole_sq = lax.psum(squares, "tp")
    scale = lax.rsqrt(whole_sq / DI + epsilon)
    return (gated.astype(F32) * scale * norm_gain).astype(BF16)


def solution(mesh):
    return jax.shard_map(
        per_device,
        mesh=mesh,
        in_specs=(
            P(None, "seq", None),
            P(None, "tp"),
            P(None, "tp"),
            P(None, "tp"),
            P(None, "tp"),
            P(None, "tp"),
            P(),
            P("tp"),
            P("tp"),
            P("tp"),
        ),
        out_specs=P(None, "seq", "tp"),
        check_vma=False,
    )
```

time: 340 us -> 150 us (0.44)
  the two profiles are of different devices: /device:TPU:7 before, /device:TPU:0 now
where the time goes in v1:
time: 150 us; the launch traced here: 149 us
  blocking collectives  44.6 us (30%)
  starting transfers between devices  34.1 us (23%)
  matrix products  29.5 us (20%)
  Pallas kernels  28.8 us (19%)
  other arithmetic  5.14 us (3%)
  local copies, waits for them, and re-layouts  4.09 us (3%)
  waiting for transfers between devices  2.45 us (2%)
    ppermute x6, starting transfers between devices, shifted(): return lax.ppermute(block, axis, route)  34.1 us
    psum x1, blocking collectives, per_device(): whole_sq = lax.psum(squares, 'tp')  26.7 us
    all_gather x1, blocking collectives, per_device(): lax.all_gather(jnp.concatenate([bc_halo, bc_part], axis=0), 'tp', axis=1,...  17.9 us
    pallas_call x1, Pallas kernels, per_device(): pl.pallas_call(state_kernel, grid=(batch,), out_shape=outs, in_specs=[one...  17.7 us
    dot_general x1, matrix products, per_device(): jnp.dot(flat, value_proj, preferred_element_type=F32).astype(BF16)  12 us
    dot_general x1, matrix products, per_device(): gate_pre = jnp.dot(flat, gate_proj, preferred_element_type=F32).astype(BF16)  11.8 us
    pallas_call x1, Pallas kernels, per_device(): pl.pallas_call(output_kernel, grid=(batch,), out_shape=outs, in_specs=[on...  11.1 us
    dot_general x1, matrix products, per_device(): jnp.dot(halo_flat, value_proj, preferred_element_type=F32).astype(BF16)  3.86 us
  transfers between devices with their start and end apart: 6, of which 2 were waited for; matrix products, arithmetic and copies ran while one was open for 18% of the time, Pallas kernels for 0%

profile of v1, /device:TPU:0, one launch (start us, length us, event | category | flops | bytes accessed | tf_op | source)
XLA Modules:
  0.0 149.1 jit_solution(2330950979061148879)
XLA Ops:
  0.0 0.9 slice.19
  0.9 2.4 %collective-permute-start = (bf16[2,8,2560]{2,1,0:T(8,128)(2,1)S(1)}, bf16[2,8,2560]{2,1,0:T(8,128)(2,1)S(1)}, u32[]{:S(2)}, u32[]{:S(2)}) collective-permute-start(bf16[2,8,2560]{2,1,0:T(8,128)(2,1)S(1)} %slice.19), channel_id=1, source_target_pairs={{0,4},{4,8},{8,12},{12,16},{16,20},{20,24},{24,28},{1,5},{5,9},{9,... | collective-permute-start | bytes 245768 | tf_op jit(solution)/shard_map/ppermute | solution.py:23
  3.4 12.0 %convolution_convert_fusion.1 = bf16[1024,1280]{1,0:T(8,128)(2,1)} fusion(bf16[1024,2560]{1,0:T(8,128)(2,1)} %bitcast.41, bf16[2560,1280]{1,0:T(8,128)(2,1)} %param.12), kind=kOutput, calls=%fused_computation.2 | convolution fusion | flops 6712197120 | bytes 14417920 | tf_op jit(solution)/shard_map/dot_general | solution.py:178
  15.4 0.1 fusion.9.expand_ref
  15.5 1.7 %convolution_bitcast_fusion = f32[1024,84]{0,1:T(8,128)S(1)} fusion(bf16[1024,2560]{1,0:T(8,128)(2,1)S(1)} %bitcast.43, bf16[2560,20]{0,1:T(8,128)(2,1)S(1)} %copy-done.9, bf16[2560,64]{0,1:T(8,128)(2,1)S(1)} %copy-done.8), kind=kOutput, calls=%fused_computation.13 | convolution fusion | flops 441262080 | bytes 6017024 | tf_op jit(solution)/shard_map/dot_general | solution.py:169
  17.2 0.2 copy.18
  17.5 0.2 convolution_convert_fusion.3
  17.6 0.1 copy.15
  17.8 0.1 pad_maximum_fusion
  17.9 17.9 %all_gather.3 = bf16[1040,256]{0,1:T(8,128)(2,1)S(1)} all-gather(bf16[1040,64]{0,1:T(8,128)(2,1)S(1)} %pad_maximum_fusion), channel_id=1, replica_groups=mesh['seq'=8,'tp'=4] {'tp'}, dimensions={1}, use_global_device_ids=true | all-gather | bytes 665600 | tf_op jit(solution)/shard_map/all_gather | solution.py:173
  35.8 0.2 slice.26
  36.0 0.2 copy.16
  36.3 3.9 %fusion.pre_halo_ref = bf16[2,8,1280]{2,1,0:T(8,128)(2,1)S(1)} fusion(bf16[2560,1280]{1,0:T(8,128)(2,1)} %param.12, bf16[2,8,2560]{2,1,0:T(8,128)(2,1)S(1)} %collective-permute-done), kind=kOutput, calls=%fused_computation.4 | convolution fusion | flops 104878080 | bytes 6676480 | tf_op jit(solution)/shard_map/dot_general | solution.py:179
  40.2 17.7 %state.1 = (bf16[2,512,1280]{2,1,0:T(8,128)(2,1)}, bf16[2,512,256]{2,1,0:T(8,128)(2,1)S(1)}, f32[2,512,20]{2,1,0:T(8,128)S(1)}, f32[2,64,20]{2,1,0:T(8,128)S(1)}...) custom-call(bf16[2,512,1280]{2,1,0:T(8,128)(2,1)} %bitcast.50, bf16[2,8,1280]{2,1,0:T(8,128)(2,1)S(1)} %fusion.pre_halo_ref, ...), custom_call_target="tpu_custom_call" | custom-call | flops 1073741824 | bytes 8388608 | tf_op jit(solution)/shard_map/state/pallas_call | solution.py:199
  58.0 0.8 copy-done
  58.8 2.4 %collective-permute-start.1 = (bf16[2,128,1280]{2,1,0:T(8,128)(2,1)S(1)}, bf16[2,128,1280]{2,1,0:T(8,128)(2,1)S(1)}, u32[]{:S(2)}, u32[]{:S(2)}) collective-permute-start(bf16[2,128,1280]{2,1,0:T(8,128)(2,1)S(1)} %convert_element_type.46), channel_id=1, source_target_pairs={{0,4},{4,8},{8,12},{12,16},{16,20},{20,24},{24,28},{1,5},{5,9},{9,... | collective-permute-start | bytes 1966088 | tf_op jit(solution)/shard_map/ppermute | solution.py:23
  61.2 1.6 %collective-permute-done.1 = bf16[2,128,1280]{2,1,0:T(8,128)(2,1)S(1)} collective-permute-done((bf16[2,128,1280]{2,1,0:T(8,128)(2,1)S(1)}, bf16[2,128,1280]{2,1,0:T(8,128)(2,1)S(1)}, u32[]{:S(2)}, u32[]{:S(2)}) %collective-permute-start.1) | collective-permute-done | bytes 655392 | tf_op jit(solution)/shard_map/ppermute | solution.py:23
  62.9 1.0 fusion.5
  63.9 11.6 %collective-permute-start.3 = (bf16[2,128,1280]{2,1,0:T(8,128)(2,1)}, bf16[2,128,1280]{2,1,0:T(8,128)(2,1)S(1)}, u32[]{:S(2)}, u32[]{:S(2)}) collective-permute-start(bf16[2,128,1280]{2,1,0:T(8,128)(2,1)} %fusion.5), channel_id=1, source_target_pairs={{0,8},{4,12},{8,16},{12,20},{16,24},{20,28},{1,9},{5,13},{9,17},{1... | collective-permute-start | bytes 1966088 | tf_op jit(solution)/shard_map/ppermute | solution.py:23
  75.5 1.3 collective-permute-start.2
  76.8 0.8 collective-permute-done.2
  77.6 14.0 %collective-permute-start.4 = (f32[2,1,1280]{2,1,0:T(1,128)S(1)}, f32[2,1,1280]{2,1,0:T(1,128)S(1)}, u32[]{:S(2)}, u32[]{:S(2)}) collective-permute-start(f32[2,1,1280]{2,1,0:T(1,128)S(1)} %get-tuple-element.21), channel_id=1, source_target_pairs={{0,8},{4,12},{8,16},{12,20},{16,24},{20,28},{1,9},{5,13},{9,17},{1... | collective-permute-start | bytes 30728 | tf_op jit(solution)/shard_map/ppermute | solution.py:23
  91.7 1.1 fusion.4
  92.8 2.3 %collective-permute-start.5 = (bf16[2,128,1280]{2,1,0:T(8,128)(2,1)}, bf16[2,128,1280]{2,1,0:T(8,128)(2,1)S(1)}, u32[]{:S(2)}, u32[]{:S(2)}) collective-permute-start(bf16[2,128,1280]{2,1,0:T(8,128)(2,1)} %fusion.4), channel_id=1, source_target_pairs={{0,16},{4,20},{8,24},{12,28},{1,17},{5,21},{9,25},{13,29},{2,18},{... | collective-permute-start | bytes 1966088 | tf_op jit(solution)/shard_map/ppermute | solution.py:23
  95.2 11.8 %convolution_convert_fusion = bf16[1024,1280]{1,0:T(8,128)(2,1)} fusion(bf16[1024,2560]{1,0:T(8,128)(2,1)} %bitcast.42, bf16[2560,1280]{1,0:T(8,128)(2,1)} %param.11), kind=kOutput, calls=%fused_computation.1 | convolution fusion | flops 6712197120 | bytes 14417920 | tf_op jit(solution)/shard_map/dot_general | solution.py:234
  107.1 0.3 fusion.2.state_ref
  107.4 0.7 copy-done.1
  108.1 11.1 %outputs.1 = (bf16[2,512,1280]{2,1,0:T(8,128)(2,1)S(1)}, f32[2,512,1]{2,1,0:T(8,128)S(1)}) custom-call(bf16[2,512,1280]{2,1,0:T(8,128)(2,1)} %get-tuple-element.13.scaled_ref, bf16[2,512,256]{2,1,0:T(8,128)(2,1)S(1)} %get-tuple-element.14.bc_ref, f32[2,512,20]{2,1,0:T(8,128)S(1)} %copy-done.1, f32[2,64,20]{2,1,0:T(8,128)S(1)} %get-tuple-element.16.em_ref, ...), custom_call_target="tpu_custom_call" | custom-call | flops 1073741824 | bytes 8388608 | tf_op jit(solution)/shard_map/outputs/pallas_call | solution.py:241
  119.2 0.8 copy-done.2
  120.0 26.7 %psum.7 = f32[2,512,1]{2,1,0:T(8,128)S(1)} all-reduce(f32[2,512,1]{2,1,0:T(8,128)} %copy-done.2), channel_id=1, replica_groups=mesh['seq'=8,'tp'=4] {'tp'}, use_global_device_ids=true, to_apply=%region_0.1 | all-reduce | flops 1024 | bytes 8192 | tf_op jit(solution)/shard_map/psum | solution.py:257
  146.7 0.2 rsqrt_reduce_fusion
  147.0 2.2 %multiply_convert_fusion = bf16[2,512,1280]{2,1,0:T(8,128)(2,1)} fusion(bf16[2,512,1280]{2,1,0:T(8,128)(2,1)S(1)} %get-tuple-element.19, f32[1280]{0:T(1024)S(1)} %copy-done.10, f32[2,512]{1,0:T(2,128)S(1)} %rsqrt_reduce_fusion), kind=kLoop, calls=%fused_computation | loop fusion | flops 5242880 | bytes 5252096 | tf_op jit(solution)/shard_map/convert_element_type | solution.py:259
  (39 shorter events, 0.3 us)
Async XLA Ops:
  0.9 16.6 %collective-permute-start = (bf16[2,8,2560]{2,1,0:T(8,128)(2,1)S(1)}, bf16[2,8,2560]{2,1,0:T(8,128)(2,1)S(1)}, u32[]{:S(2)}, u32[]{:S(2)}) collective-permute-start(bf16[2,8,2560]{2,1,0:T(8,128)(2,1)S(1)} %slice.19), channel_id=1, source_target_pairs={{0,4},{4,8},{8,12},{12,16},{16,20},{20,24},{24,28},{1,5},{5,9},{9,... | collective-permute-start | bytes 245768 | tf_op jit(solution)/shard_map/ppermute | solution.py:23
  3.4 12.1 %copy-start.7 = (bf16[2,512,2560]{2,1,0:T(8,128)(2,1)S(1)}, bf16[2,512,2560]{2,1,0:T(8,128)(2,1)}, u32[]{:S(2)}) copy-start(bf16[2,512,2560]{2,1,0:T(8,128)(2,1)} %param.10) | copy-start | bytes 15728644
  3.4 12.1 %copy-start.8 = (bf16[2560,64]{0,1:T(8,128)(2,1)S(1)}, bf16[2560,64]{0,1:T(8,128)(2,1)}, u32[]{:S(2)}) copy-start(bf16[2560,64]{0,1:T(8,128)(2,1)} %param.13) | copy-start | bytes 983044
  3.4 12.1 %copy-start.9 = (bf16[2560,20]{0,1:T(8,128)(2,1)S(1)}, bf16[2560,20]{0,1:T(8,128)(2,1)}, u32[]{:S(2)}) copy-start(bf16[2560,20]{0,1:T(8,128)(2,1)} %param.14) | copy-start | bytes 307204
  36.3 3.9 %copy-start.3 = (f32[4,1280]{1,0:T(4,128)S(1)}, f32[4,1280]{1,0:T(4,128)}, u32[]{:S(2)}) copy-start(f32[4,1280]{1,0:T(4,128)} %kernel_ref.1) | copy-start | bytes 61444
  36.3 3.9 %copy-start.4 = (f32[4,256]{1,0:T(4,128)S(1)}, f32[4,256]{1,0:T(4,128)}, u32[]{:S(2)}) copy-start(f32[4,256]{1,0:T(4,128)} %bc_kernel_ref.1) | copy-start | bytes 12292
  36.3 3.9 %copy-start.5 = (f32[20]{0:T(128)S(1)}, f32[20]{0:T(128)}, u32[]{:S(2)}) copy-start(f32[20]{0:T(128)} %param.17) | copy-start | bytes 244
  36.3 3.9 %copy-start.6 = (f32[20]{0:T(128)S(1)}, f32[20]{0:T(128)}, u32[]{:S(2)}) copy-start(f32[20]{0:T(128)} %param.18) | copy-start | bytes 244
  58.0 0.8 copy-start
  58.8 4.0 %collective-permute-start.1 = (bf16[2,128,1280]{2,1,0:T(8,128)(2,1)S(1)}, bf16[2,128,1280]{2,1,0:T(8,128)(2,1)S(1)}, u32[]{:S(2)}, u32[]{:S(2)}) collective-permute-start(bf16[2,128,1280]{2,1,0:T(8,128)(2,1)S(1)} %convert_element_type.46), channel_id=1, source_target_pairs={{0,4},{4,8},{8,12},{12,16},{16,20},{20,24},{24,28},{1,5},{5,9},{9,... | collective-permute-start | bytes 1966088 | tf_op jit(solution)/shard_map/ppermute | solution.py:23
  63.9 27.8 %collective-permute-start.3 = (bf16[2,128,1280]{2,1,0:T(8,128)(2,1)}, bf16[2,128,1280]{2,1,0:T(8,128)(2,1)S(1)}, u32[]{:S(2)}, u32[]{:S(2)}) collective-permute-start(bf16[2,128,1280]{2,1,0:T(8,128)(2,1)} %fusion.5), channel_id=1, source_target_pairs={{0,8},{4,12},{8,16},{12,20},{16,24},{20,28},{1,9},{5,13},{9,17},{1... | collective-permute-start | bytes 1966088 | tf_op jit(solution)/shard_map/ppermute | solution.py:23
  75.5 2.1 %collective-permute-start.2 = (f32[2,1,1280]{2,1,0:T(1,128)S(1)}, f32[2,1,1280]{2,1,0:T(1,128)S(1)}, u32[]{:S(2)}, u32[]{:S(2)}) collective-permute-start(f32[2,1,1280]{2,1,0:T(1,128)S(1)} %slice.24), channel_id=1, source_target_pairs={{0,4},{4,8},{8,12},{12,16},{16,20},{20,24},{24,28},{1,5},{5,9},{9,... | collective-permute-start | bytes 30728 | tf_op jit(solution)/shard_map/ppermute | solution.py:23
  77.6 29.4 %collective-permute-start.4 = (f32[2,1,1280]{2,1,0:T(1,128)S(1)}, f32[2,1,1280]{2,1,0:T(1,128)S(1)}, u32[]{:S(2)}, u32[]{:S(2)}) collective-permute-start(f32[2,1,1280]{2,1,0:T(1,128)S(1)} %get-tuple-element.21), channel_id=1, source_target_pairs={{0,8},{4,12},{8,16},{12,20},{16,24},{20,28},{1,9},{5,13},{9,17},{1... | collective-permute-start | bytes 30728 | tf_op jit(solution)/shard_map/ppermute | solution.py:23
  92.8 14.2 %collective-permute-start.5 = (bf16[2,128,1280]{2,1,0:T(8,128)(2,1)}, bf16[2,128,1280]{2,1,0:T(8,128)(2,1)S(1)}, u32[]{:S(2)}, u32[]{:S(2)}) collective-permute-start(bf16[2,128,1280]{2,1,0:T(8,128)(2,1)} %fusion.4), channel_id=1, source_target_pairs={{0,16},{4,20},{8,24},{12,28},{1,17},{5,21},{9,25},{13,29},{2,18},{... | collective-permute-start | bytes 1966088 | tf_op jit(solution)/shard_map/ppermute | solution.py:23
  107.0 1.0 copy-start.1
  108.1 38.9 %copy-start.10 = (f32[1280]{0:T(1024)S(1)}, f32[1280]{0:T(1024)}, u32[]{:S(2)}) copy-start(f32[1280]{0:T(1024)} %param.19) | copy-start | bytes 15364
  119.2 0.8 copy-start.2

commit v2 on v1

v2 whole, which is shorter than its diff:
```python
import jax
import jax.numpy as jnp
from jax import lax
from jax.experimental import pallas as pl
from jax.experimental.pallas import tpu as pltpu
from jax.sharding import PartitionSpec as P

DI = 5120
HEAD_DIM = 64
STATE = 128
CONV = 4
BLOCK = 64
PAD = 16
FIRST = PAD - CONV + 1
MESH = pl.DeviceIdType.MESH

epsilon = 1e-05
F32 = jnp.float32
BF16 = jnp.bfloat16


def shifted(block, axis, distance):
    count = lax.axis_size(axis)
    route = [(i, i + distance) for i in range(count - distance)]
    return lax.ppermute(block, axis, route)


def silu(x):
    return x * (1.0 / (1.0 + jnp.exp(-x)))


def spread(x, expand):
    high = x.astype(BF16)
    low = (x - high.astype(F32)).astype(BF16)
    return jnp.dot(jnp.concatenate([high, low], axis=1), expand, preferred_element_type=F32)


def tile_of(width):
    return 256 if width % 256 == 0 else 128


def state_kernel(
    pre_ref, bc_ref, step_ref, kernel_ref, bc_kernel_ref,
    bias_ref, rate_ref, expand_ref,
    scaled_ref, bc_out_ref, fout_ref, em_ref, state_out_ref, decay_ref,
    window, bc_window, lows, state_ref,
):
    length, width = step_ref.shape[1], pre_ref.shape[2]
    tile = tile_of(width)
    window[0:PAD, :] = pre_ref[0, 0:PAD, :].astype(F32)
    bc_window[0:PAD, :] = bc_ref[0, 0:PAD, :].astype(F32)
    state_ref[...] = jnp.zeros_like(state_ref)
    heads = bias_ref.shape[1]
    rows = lax.broadcasted_iota(jnp.int32, (BLOCK, BLOCK), 0)
    cols = lax.broadcasted_iota(jnp.int32, (BLOCK, BLOCK), 1)
    triangle = jnp.where(rows >= cols, 1.0, 0.0).astype(F32)
    lows[...] = jnp.zeros_like(lows)

    @pl.loop(0, length // BLOCK)
    def _(index):
        at = pl.ds(pl.multiple_of(index * BLOCK, BLOCK), BLOCK)
        past = pl.ds(pl.multiple_of(index * BLOCK + PAD, PAD), BLOCK)
        step_pre = step_ref[0, at, :] + bias_ref[...]
        steps = jnp.maximum(step_pre, 0.0) + jnp.log1p(jnp.exp(-jnp.abs(step_pre)))
        log_decay = -steps * jnp.exp(rate_ref[...])
        cumulative = jnp.dot(
            triangle, log_decay, precision=lax.Precision.HIGHEST, preferred_element_type=F32
        )
        last = cumulative[BLOCK - 1 : BLOCK, :]
        lows[0:1, :] += last
        mid = 0.5 * last
        fin = jnp.exp(mid - cumulative) * steps
        fout_ref[0, at, :] = jnp.exp(cumulative - mid)
        em = jnp.broadcast_to(jnp.exp(mid), (8, heads))
        em_ref[0, pl.ds(pl.multiple_of(index * 8, 8), 8), :] = em
        wide_fin = spread(fin, expand_ref[...])
        wide_em = spread(em, expand_ref[...])[0:1, :]

        bc_window[PAD:, :] = bc_ref[0, past, :].astype(F32)
        bc = bc_kernel_ref[0:1, :] * bc_window[FIRST : FIRST + BLOCK, :]
        for k in range(1, CONV):
            bc = bc + bc_kernel_ref[k : k + 1, :] * bc_window[FIRST + k : FIRST + k + BLOCK, :]
        bc = silu(bc).astype(BF16)
        bc_out_ref[0, at, :] = bc
        bc_window[0:PAD, :] = bc_window[BLOCK : BLOCK + PAD, :]
        b_rows = bc[:, :STATE]

        for start in range(0, width, tile):
            cut = slice(start, start + tile)
            window[PAD:, cut] = pre_ref[0, past, cut].astype(F32)
            x = kernel_ref[0:1, cut] * window[FIRST : FIRST + BLOCK, cut]
            for k in range(1, CONV):
                x = x + kernel_ref[k : k + 1, cut] * window[FIRST + k : FIRST + k + BLOCK, cut]
            scaled = (silu(x) * wide_fin[:, cut]).astype(BF16)
            window[0:PAD, cut] = window[BLOCK : BLOCK + PAD, cut]
            scaled_ref[0, at, cut] = scaled
            added = lax.dot_general(
                b_rows, scaled, (((0,), (0,)), ((), ())), preferred_element_type=F32
            )
            e = wide_em[:, cut]
            state_ref[:, cut] = e * (e * state_ref[:, cut] + added)

    state_out_ref[0] = state_ref[...].astype(BF16)
    decay_ref[0] = spread(jnp.exp(lows[...]), expand_ref[...])


def value_kernel(
    hidden_ref, halo_ref, bc_ref, weight_ref,
    pre_ref, bc_out_ref,
    rows, slots, load_sem, send_sem, recv_sem,
):
    batch = hidden_ref.shape[0]
    count = slots.shape[0]
    narrow = bc_ref.shape[1]
    me = lax.axis_index("tp")
    step = pl.program_id(0)

    def sends():
        for away in range(1, count):
            peer = lax.rem(me + away, count)
            yield pltpu.make_async_remote_copy(
                src_ref=bc_ref, dst_ref=slots.at[me],
                send_sem=send_sem.at[away - 1], recv_sem=recv_sem.at[away - 1],
                device_id={"tp": peer}, device_id_type=MESH,
            )

    @pl.when(step == 0)
    def _():
        loads = []
        for b in range(batch):
            loads.append(pltpu.make_async_copy(
                hidden_ref.at[b], rows.at[b, pl.ds(PAD, hidden_ref.shape[1])], load_sem.at[2 * b]
            ))
            loads.append(pltpu.make_async_copy(
                halo_ref.at[b], rows.at[b, pl.ds(0, PAD)], load_sem.at[2 * b + 1]
            ))
        loads.append(pltpu.make_async_copy(bc_ref, slots.at[me], load_sem.at[2 * batch]))
        for load in loads:
            load.start()
        barrier = pltpu.get_barrier_semaphore()
        for away in range(1, count):
            pl.semaphore_signal(
                barrier, inc=1, device_id={"tp": lax.rem(me + away, count)}, device_id_type=MESH
            )
        pl.semaphore_wait(barrier, count - 1)
        for send in sends():
            send.start()
        for load in loads:
            load.wait()

    @pl.loop(0, batch)
    def _(b):
        pre_ref[b] = jnp.dot(
            rows[b], weight_ref[...], preferred_element_type=F32
        ).astype(BF16)

    @pl.when(step == pl.num_programs(0) - 1)
    def _():
        for send in sends():
            send.wait()
        bc_out_ref[...] = jnp.concatenate([slots[k] for k in range(count)], axis=1)


def gate_kernel(
    hidden_ref, weight_ref, local_ref, span_ref,
    gate_ref, before_ref,
    pair, pair_span, sent, sent_span, got, got_span, entering, entering_half, reach,
    send_sem, recv_sem,
):
    step = pl.program_id(0)
    place = lax.axis_index("seq")
    chips = lax.axis_size("seq") // 2
    core = lax.rem(place, 2)
    chip = place // 2
    partner = place + 1 - 2 * core
    half = STATE // 2
    batch = local_ref.shape[0]
    mine = pl.ds(pl.multiple_of(core * half, half), half)
    distances = []
    while 2 ** len(distances) < chips:
        distances.append(2 ** len(distances))

    def copies(source, target, slot, device):
        return pltpu.make_async_remote_copy(
            src_ref=source, dst_ref=target, send_sem=send_sem.at[slot],
            recv_sem=recv_sem.at[slot], device_id={"seq": device}, device_id_type=MESH,
        )

    def pair_copies():
        return (copies(local_ref, pair, 0, partner), copies(span_ref, pair_span, 1, partner))

    def round_copies(r):
        device = lax.rem(place + 2 * distances[r], 2 * chips)
        return (
            copies(sent.at[r], got.at[r], 2 + 2 * r, device),
            copies(sent_span.at[r], got_span.at[r], 3 + 2 * r, device),
        )

    @pl.when(step == 0)
    def _():
        barrier = pltpu.get_barrier_semaphore()
        pl.semaphore_signal(barrier, inc=1, device_id={"seq": partner}, device_id_type=MESH)
        for d in distances:
            for away in (2 * d, 2 * (chips - d)):
                pl.semaphore_signal(
                    barrier, inc=1, device_id={"seq": lax.rem(place + away, 2 * chips)},
                    device_id_type=MESH,
                )
        pl.semaphore_wait(barrier, 1 + 2 * len(distances))
        for copy in pair_copies():
            copy.start()

    def start_round(r):
        @pl.when(chip + distances[r] < chips)
        def _():
            for copy in round_copies(r):
                copy.start()

    @pl.when(step == 1)
    def _():
        for copy in pair_copies():
            copy.wait()
        sent_span[0] = span_ref[...] * pair_span[...]
        reach[...] = jnp.ones_like(reach)
        for b in range(batch):
            own = local_ref[b, mine, :].astype(F32)
            other = pair[b, mine, :].astype(F32)
            first = jnp.where(core == 0, own, other)
            second = jnp.where(core == 0, other, own)
            later = jnp.where(core == 0, pair_span[b : b + 1, :], span_ref[b : b + 1, :])
            sent[0, b] = (later * first + second).astype(BF16)
            entering_half[b] = jnp.zeros((half, own.shape[1]), BF16)
        start_round(0)

    gate_ref[...] = jnp.dot(
        hidden_ref[...], weight_ref[...], preferred_element_type=F32
    ).astype(BF16)

    @pl.when(step == pl.num_programs(0) - 1)
    def _():
        for r, d in enumerate(distances):
            @pl.when(chip + d < chips)
            def _():
                for copy in round_copies(r):
                    copy.wait_send()

            more = r + 1 < len(distances)

            @pl.when(chip >= d)
            def _():
                for copy in round_copies(r):
                    copy.wait_recv()
                for b in range(batch):
                    arrived = got[r, b].astype(F32)
                    entering_half[b] = (
                        entering_half[b].astype(F32) + reach[b : b + 1, :] * arrived
                    ).astype(BF16)
                    if more:
                        sent[r + 1, b] = (
                            sent[r, b].astype(F32) + sent_span[r, b : b + 1, :] * arrived
                        ).astype(BF16)
                reach[...] = reach[...] * got_span[r]
                if more:
                    sent_span[r + 1] = sent_span[r] * got_span[r]

            if more:
                @pl.when(chip < d)
                def _():
                    sent[r + 1] = sent[r]
                    sent_span[r + 1] = sent_span[r]

                start_round(r + 1)
        last = 2 + 2 * len(distances)
        swap = copies(entering_half, entering.at[:, mine, :], last, partner)
        swap.start()
        swap.wait()
        for b in range(batch):
            entering[b, mine, :] = entering_half[b]
        for b in range(batch):
            full = entering[b].astype(F32)
            moved = pair_span[b : b + 1, :] * full + pair[b].astype(F32)
            before_ref[b] = jnp.where(core == 0, full, moved)


def output_kernel(
    scaled_ref, bc_ref, fout_ref, em_ref, state_ref, gate_ref, expand_ref, gain_ref,
    out_ref,
    held, right, gated_all, sums, others, send_sem, recv_sem,
):
    length, width = scaled_ref.shape[1], scaled_ref.shape[2]
    blocks = length // BLOCK
    tile = tile_of(width)
    step = pl.program_id(0)
    batch = pl.num_programs(0) // 2
    rows = lax.broadcasted_iota(jnp.int32, (BLOCK, BLOCK), 0)
    cols = lax.broadcasted_iota(jnp.int32, (BLOCK, BLOCK), 1)
    lane = lax.broadcasted_iota(jnp.int32, (BLOCK, 128), 1)
    count = others.shape[0] + 1
    me = lax.axis_index("tp")

    def sends():
        for away in range(1, count):
            yield pltpu.make_async_remote_copy(
                src_ref=sums, dst_ref=others.at[away - 1],
                send_sem=send_sem.at[away - 1], recv_sem=recv_sem.at[away - 1],
                device_id={"tp": lax.rem(me + away, count)}, device_id_type=MESH,
            )

    @pl.when(step == 0)
    def _():
        sums[...] = jnp.zeros_like(sums)
        barrier = pltpu.get_barrier_semaphore()
        for away in range(1, count):
            pl.semaphore_signal(
                barrier, inc=1, device_id={"tp": lax.rem(me + away, count)}, device_id_type=MESH
            )
        pl.semaphore_wait(barrier, count - 1)

    @pl.when(step < batch)
    def _():
        held[...] = state_ref[0]

        @pl.loop(0, blocks)
        def _(index):
            at = pl.ds(pl.multiple_of(index * BLOCK, BLOCK), BLOCK)
            wide_fout = spread(fout_ref[0, at, :], expand_ref[...])
            em = em_ref[0, pl.ds(pl.multiple_of(index * 8, 8), 8), :]
            wide_em = spread(em, expand_ref[...])[0:1, :]
            b_rows = bc_ref[0, at, :STATE]
            c_rows = bc_ref[0, at, STATE:]
            scores = lax.dot_general(
                c_rows, b_rows, (((1,), (1,)), ((), ())), preferred_element_type=F32
            )
            mixing = jnp.where(rows >= cols, scores, 0.0).astype(BF16)
            left = jnp.concatenate([c_rows, mixing], axis=1)
            total = jnp.zeros((BLOCK, 128), F32)
            for start in range(0, width, tile):
                cut = slice(start, start + tile)
                scaled = scaled_ref[0, at, cut]
                e = wide_em[:, cut]
                entering = e * held[:, cut]
                right[:STATE, cut] = entering.astype(BF16)
                right[STATE:, cut] = scaled
                y = jnp.dot(left, right[:, cut], preferred_element_type=F32)
                added = lax.dot_general(
                    b_rows, scaled, (((0,), (0,)), ((), ())), preferred_element_type=F32
                )
                held[:, cut] = e * (entering + added)
                gated = y * wide_fout[:, cut] * silu(gate_ref[0, at, cut].astype(F32))
                gated_all[step, at, cut] = gated
                squared = gated * gated
                for piece in range(0, tile, 128):
                    total = total + squared[:, piece : piece + 128]
            column = jnp.sum(total, axis=1, keepdims=True)
            sums[...] += jnp.where(lane == step * blocks + index, column, 0.0)

    @pl.when(step == batch - 1)
    def _():
        for send in sends():
            send.start()

    @pl.when(step == batch)
    def _():
        for send in sends():
            send.wait()

    @pl.when(step >= batch)
    def _():
        whole_sq = sums[...]
        for away in range(1, count):
            whole_sq = whole_sq + others[away - 1]
        scale = lax.rsqrt(whole_sq / DI + epsilon)

        @pl.loop(0, blocks)
        def _(index):
            at = pl.ds(pl.multiple_of(index * BLOCK, BLOCK), BLOCK)
            here = (step - batch) * blocks + index
            column = jnp.sum(jnp.where(lane == here, scale, 0.0), axis=1, keepdims=True)
            for start in range(0, width, tile):
                cut = slice(start, start + tile)
                out_ref[0, at, cut] = (
                    gated_all[step - batch, at, cut] * column * gain_ref[:, cut]
                ).astype(BF16)


def one_batch(shape):
    return pl.BlockSpec((1,) + tuple(shape[1:]), lambda b: (b,) + (0,) * (len(shape) - 1))


def whole(shape):
    return pl.BlockSpec(tuple(shape), lambda b: (0,) * len(shape))


def per_device(
    hidden_in, gate_proj, value_proj, bc_proj, step_proj,
    value_conv, bc_conv, step_bias, log_rate, norm_gain,
):
    batch, length, model_width = hidden_in.shape
    heads = step_proj.shape[1]
    width = value_proj.shape[1]
    narrow = bc_proj.shape[1]
    blocks = length // BLOCK
    tp = lax.axis_size("tp")
    tile = tile_of(width)
    flat = hidden_in.reshape(-1, model_width)
    halo_in = shifted(hidden_in[:, length - PAD :, :], "seq", 1)

    small = jnp.concatenate([bc_proj, step_proj], axis=1)
    small_pre = jnp.dot(flat, small, preferred_element_type=F32)
    step_pre = small_pre[:, narrow:].reshape(batch, length, heads)
    bc_part = small_pre[:, :narrow].astype(BF16).reshape(batch, length, narrow)
    bc_halo = jnp.dot(
        halo_in.reshape(-1, model_width), bc_proj, preferred_element_type=F32
    ).astype(BF16).reshape(batch, PAD, narrow)
    bc_part = jnp.concatenate([bc_halo, bc_part], axis=1).reshape(-1, narrow)
    hbm = pl.BlockSpec(memory_space=pl.ANY)
    padded = PAD + length
    value_pre, bc_pre = pl.pallas_call(
        value_kernel,
        grid=(width // tile,),
        out_shape=(
            jax.ShapeDtypeStruct((batch, padded, width), BF16),
            jax.ShapeDtypeStruct((batch * padded, narrow * tp), BF16),
        ),
        in_specs=[hbm, hbm, hbm, pl.BlockSpec((model_width, tile), lambda j: (0, j))],
        out_specs=[
            pl.BlockSpec((batch, padded, tile), lambda j: (0, 0, j)),
            pl.BlockSpec((batch * padded, narrow * tp), lambda j: (0, 0)),
        ],
        scratch_shapes=[
            pltpu.VMEM((batch, padded, model_width), BF16),
            pltpu.VMEM((tp, batch * padded, narrow), BF16),
            pltpu.SemaphoreType.DMA((2 * batch + 1,)),
            pltpu.SemaphoreType.DMA((tp - 1,)),
            pltpu.SemaphoreType.DMA((tp - 1,)),
        ],
        compiler_params=pltpu.CompilerParams(
            vmem_limit_bytes=48 << 20, collective_id=0, has_side_effects=True
        ),
        name="value",
    )(hidden_in, halo_in, bc_part, value_proj)
    bc_pre = bc_pre.reshape(batch, padded, narrow * tp)

    lanes = lax.broadcasted_iota(jnp.int32, (2 * heads, width), 1) // HEAD_DIM
    owner = lax.broadcasted_iota(jnp.int32, (2 * heads, width), 0) % heads
    expand = (lanes == owner).astype(BF16)
    bias = step_bias.reshape(1, heads)
    rate = log_rate.reshape(1, heads)

    ins = (value_pre, bc_pre, step_pre)
    fixed = (value_conv, bc_conv, bias, rate, expand)
    outs = (
        jax.ShapeDtypeStruct((batch, length, width), BF16),
        jax.ShapeDtypeStruct((batch, length, 2 * STATE), BF16),
        jax.ShapeDtypeStruct((batch, length, heads), F32),
        jax.ShapeDtypeStruct((batch, blocks * 8, heads), F32),
        jax.ShapeDtypeStruct((batch, STATE, width), BF16),
        jax.ShapeDtypeStruct((batch, 8, width), F32),
    )
    scaled, bc, fout, em, local_state, decay = pl.pallas_call(
        state_kernel,
        grid=(batch,),
        out_shape=outs,
        in_specs=[one_batch(a.shape) for a in ins] + [whole(a.shape) for a in fixed],
        out_specs=[one_batch(a.shape) for a in outs],
        scratch_shapes=[
            pltpu.VMEM((BLOCK + PAD, width), F32),
            pltpu.VMEM((BLOCK + PAD, 2 * STATE), F32),
            pltpu.VMEM((8, heads), F32),
            pltpu.VMEM((STATE, width), F32),
        ],
        compiler_params=pltpu.CompilerParams(vmem_limit_bytes=48 << 20),
        cost_estimate=pl.CostEstimate(
            flops=1 << 30, bytes_accessed=8 << 20, transcendentals=1 << 21
        ),
        name="state",
    )(*ins, *fixed)

    span = jnp.concatenate([decay[:, 0, :], decay[: 8 - batch, 1, :]], axis=0)
    span = jnp.pad(span, ((0, 8 - span.shape[0]), (0, 0)))
    chips = lax.axis_size("seq") // 2
    rounds = max(1, (chips - 1).bit_length())
    half = STATE // 2
    moves = 3 + 2 * rounds
    once = pl.Buffered(1)
    gate_pre, before = pl.pallas_call(
        gate_kernel,
        grid=(width // tile,),
        out_shape=(
            jax.ShapeDtypeStruct((batch * length, width), BF16),
            jax.ShapeDtypeStruct((batch, STATE, width), F32),
        ),
        in_specs=[
            pl.BlockSpec(flat.shape, lambda j: (0, 0), pipeline_mode=once),
            pl.BlockSpec((model_width, tile), lambda j: (0, j)),
            pl.BlockSpec(local_state.shape, lambda j: (0, 0, 0), pipeline_mode=once),
            pl.BlockSpec(span.shape, lambda j: (0, 0), pipeline_mode=once),
        ],
        out_specs=[
            pl.BlockSpec((batch * length, tile), lambda j: (0, j)),
            pl.BlockSpec((batch, STATE, width), lambda j: (0, 0, 0)),
        ],
        scratch_shapes=[
            pltpu.VMEM((batch, STATE, width), BF16),
            pltpu.VMEM((8, width), F32),
            pltpu.VMEM((rounds, batch, half, width), BF16),
            pltpu.VMEM((rounds, 8, width), F32),
            pltpu.VMEM((rounds, batch, half, width), BF16),
            pltpu.VMEM((rounds, 8, width), F32),
            pltpu.VMEM((batch, STATE, width), BF16),
            pltpu.VMEM((batch, half, width), BF16),
            pltpu.VMEM((8, width), F32),
            pltpu.SemaphoreType.DMA((moves,)),
            pltpu.SemaphoreType.DMA((moves,)),
        ],
        compiler_params=pltpu.CompilerParams(
            vmem_limit_bytes=56 << 20, collective_id=1, has_side_effects=True
        ),
        name="gate",
    )(flat, gate_proj, local_state, span)
    gate_pre = gate_pre.reshape(batch, length, width)

    ins = (scaled, bc, fout, em, before, gate_pre)

    def clamped(shape):
        return pl.BlockSpec(
            (1,) + tuple(shape[1:]), lambda s: (jnp.minimum(s, batch - 1), 0, 0)
        )

    gain = norm_gain.reshape(1, width)
    return pl.pallas_call(
        output_kernel,
        grid=(2 * batch,),
        out_shape=jax.ShapeDtypeStruct((batch, length, width), BF16),
        in_specs=[clamped(a.shape) for a in ins] + [whole(expand.shape), whole(gain.shape)],
        out_specs=pl.BlockSpec(
            (1, length, width), lambda s: (jnp.maximum(s - batch, 0), 0, 0)
        ),
        scratch_shapes=[
            pltpu.VMEM((STATE, width), F32),
            pltpu.VMEM((STATE + BLOCK, width), BF16),
            pltpu.VMEM((batch, length, width), F32),
            pltpu.VMEM((BLOCK, 128), F32),
            pltpu.VMEM((tp - 1, BLOCK, 128), F32),
            pltpu.SemaphoreType.DMA((tp - 1,)),
            pltpu.SemaphoreType.DMA((tp - 1,)),
        ],
        compiler_params=pltpu.CompilerParams(
            vmem_limit_bytes=56 << 20, collective_id=2, has_side_effects=True
        ),
        name="outputs",
    )(*ins, expand, gain)


def solution(mesh):
    return jax.shard_map(
        per_device,
        mesh=mesh,
        in_specs=(
            P(None, "seq", None),
            P(None, "tp"),
            P(None, "tp"),
            P(None, "tp"),
            P(None, "tp"),
            P(None, "tp"),
            P(),
            P("tp"),
            P("tp"),
            P("tp"),
        ),
        out_specs=P(None, "seq", "tp"),
        check_vma=False,
    )
```

time: 150 us -> 116 us (0.77)
  the two profiles are of different devices: /device:TPU:0 before, /device:TPU:7 now
where the time goes in v2:
time: 116 us
  Pallas kernels  97.3 us (84%)
  local copies, waits for them, and re-layouts  11.5 us (10%)
  matrix products  4.58 us (4%)
  starting transfers between devices  1.29 us (1%)
    pallas_call x1, Pallas kernels, per_device(): pl.pallas_call(gate_kernel, grid=(width // tile,), out_shape=(jax.ShapeDt...  30.8 us
    pallas_call x1, Pallas kernels, per_device(): pl.pallas_call(output_kernel, grid=(2 * batch,), out_shape=jax.ShapeDtype...  26.1 us
    pallas_call x1, Pallas kernels, per_device(): pl.pallas_call(value_kernel, grid=(width // tile,), out_shape=(jax.ShapeD...  23.6 us
    pallas_call x1, Pallas kernels, per_device(): pl.pallas_call(state_kernel, grid=(batch,), out_shape=outs, in_specs=[one...  16.8 us
    unnamed x27, local copies, waits for them, and re-layouts  9.47 us
    dot_general x1, matrix products, per_device(): small_pre = jnp.dot(flat, small, preferred_element_type=F32)  4.38 us
  transfers between devices with their start and end apart: 1, of which 0 were waited for; matrix products, arithmetic and copies ran while one was open for 5% of the time, Pallas kernels for 0%

profile of v2, /device:TPU:7, one launch (start us, length us, event | category | flops | bytes accessed | tf_op | source)
XLA Modules:
  0.0 115.8 jit_solution(16394672293549350191)
XLA Ops:
  0.0 1.0 slice.16
  1.0 1.3 %collective-permute-start = (bf16[2,16,2560]{2,1,0:T(8,128)(2,1)S(1)}, bf16[2,16,2560]{2,1,0:T(8,128)(2,1)S(1)}, u32[]{:S(2)}, u32[]{:S(2)}) collective-permute-start(bf16[2,16,2560]{2,1,0:T(8,128)(2,1)S(1)} %slice.16), channel_id=1, source_target_pairs={{0,4},{4,8},{8,12},{12,16},{16,20},{20,24},{24,28},{1,5},{5,9},{9,... | collective-permute-start | bytes 491528 | tf_op jit(solution)/shard_map/ppermute | solution.py:25
  2.3 0.1 fusion.3.expand_ref
  2.5 0.0 copy-start.4
  2.5 4.4 %convolution_bitcast_fusion = f32[1024,84]{0,1:T(8,128)S(1)} fusion(bf16[1024,2560]{1,0:T(8,128)(2,1)} %bitcast.25, bf16[2560,20]{0,1:T(8,128)(2,1)} %param.14, bf16[2560,64]{0,1:T(8,128)(2,1)} %param.13), kind=kOutput, calls=%fused_computation | convolution fusion | flops 441262080 | bytes 6017024 | tf_op jit(solution)/shard_map/dot_general | solution.py:409
  6.9 0.0 copy-done.12
  6.9 0.6 reshape.43.gain_ref
  7.5 0.2 copy.15
  7.7 0.2 copy.12
  7.9 0.0 collective-permute-done.halo_ref
  7.9 0.0 copy-done.11
  7.9 0.2 convolution_convert_fusion
  8.1 0.1 pad_maximum_fusion
  8.2 0.0 copy-start.7
  8.2 0.0 copy-start.8
  8.2 0.0 copy-start.9
  8.2 0.0 copy-start.10
  8.3 23.6 %value.1 = (bf16[2,528,1280]{2,1,0:T(8,128)(2,1)S(1)}, bf16[1056,256]{1,0:T(8,128)(2,1)S(1)}) custom-call(bf16[2,512,2560]{2,1,0:T(8,128)(2,1)} %hidden_ref.1, bf16[2,16,2560]{2,1,0:T(8,128)(2,1)S(1)} %collective-permute-done.halo_ref, bf16[1056,64]{1,0:T(8,128)(2,1)S(1)} %bitcast.19, bf16[2560,1280]{1,0:T(8,128)(2,1)} %weight_ref.2), custom_call_target="tpu_custom_call" | custom-call | tf_op jit(solution)/shard_map/value/pallas_call | solution.py:418
  31.9 0.0 copy-start.6
  31.9 1.5 %copy-done.6 = bf16[2,528,1280]{2,1,0:T(8,128)(2,1)} copy-done((bf16[2,528,1280]{2,1,0:T(8,128)(2,1)}, bf16[2,528,1280]{2,1,0:T(8,128)(2,1)S(1)}, u32[]{:S(2)}) %copy-start.6) | copy-done | bytes 2703384
  33.4 0.0 copy-done.4
  33.4 0.0 copy-done.10
  33.4 16.8 %state.1 = (bf16[2,512,1280]{2,1,0:T(8,128)(2,1)S(1)}, bf16[2,512,256]{2,1,0:T(8,128)(2,1)S(1)}, f32[2,512,20]{2,1,0:T(8,128)S(1)}, f32[2,64,20]{2,1,0:T(8,128)S...) custom-call(bf16[2,528,1280]{2,1,0:T(8,128)(2,1)} %copy-done.6, bf16[2,528,256]{2,1,0:T(8,128)(2,1)S(1)} %bitcast.22, ...), custom_call_target="tpu_custom_call" | custom-call | flops 1073741824 | bytes 8388608 | tf_op jit(solution)/shard_map/state/pallas_call | solution.py:460
  50.2 1.5 %copy-done = bf16[2,512,1280]{2,1,0:T(8,128)(2,1)} copy-done((bf16[2,512,1280]{2,1,0:T(8,128)(2,1)}, bf16[2,512,1280]{2,1,0:T(8,128)(2,1)S(1)}, u32[]{:S(2)}) %copy-start) | copy-done | bytes 2621464
  51.7 0.8 copy-done.1
  52.6 0.8 copy-done.2
  53.4 0.8 copy-done.3
  54.2 0.6 copy-done.5
  54.8 0.6 select_maximum_fusion.span_ref
  55.4 30.8 %gate.1 = (bf16[1024,1280]{1,0:T(8,128)(2,1)}, f32[2,128,1280]{2,1,0:T(8,128)}) custom-call(bf16[1024,2560]{1,0:T(8,128)(2,1)} %bitcast.26, bf16[2560,1280]{1,0:T(8,128)(2,1)} %weight_ref.3, bf16[2,128,1280]{2,1,0:T(8,128)(2,1)} %copy-done.1, f32[8,1280]{1,0:T(8,128)} %select_maximum_fusion.span_ref), custom_call_target="tpu_custom_call" | custom-call | tf_op jit(solution)/shard_map/gate/pallas_call | solution.py:486
  86.2 26.1 %outputs.1 = bf16[2,512,1280]{2,1,0:T(8,128)(2,1)} custom-call(bf16[2,512,1280]{2,1,0:T(8,128)(2,1)} %copy-done, bf16[2,512,256]{2,1,0:T(8,128)(2,1)} %copy-done.2, f32[2,512,20]{2,1,0:T(8,128)} %copy-done.3, f32[2,64,20]{2,1,0:T(8,128)} %copy-done.5, f32[2,128,1280]{2,1,0:T(8,128)} %get-tuple-element.23.state_ref, bf16[2,512,1280]{2,1,0:T(8,128)(2,1)} %bitcast.27, ...), custom_call_target="tpu_custom_call" | custom-call | tf_op jit(solution)/shard_map/outputs/pallas_call | solution.py:531
  112.4 3.4 %copy.17 = bf16[2,512,1280]{2,1,0:T(8,128)(2,1)} copy(bf16[2,512,1280]{2,1,0:T(8,128)(2,1)} %outputs.1) | data formatting | bytes 5242880
  (18 shorter events, 0.1 us)
Async XLA Ops:
  0.0 7.9 %copy-start.11 = (bf16[2560,64]{0,1:T(8,128)(2,1)S(1)}, bf16[2560,64]{0,1:T(8,128)(2,1)}, u32[]{:S(2)}) copy-start(bf16[2560,64]{0,1:T(8,128)(2,1)} %param.13) | copy-start | bytes 983044
  0.0 6.9 %copy-start.12 = (f32[1280]{0:T(1024)S(1)}, f32[1280]{0:T(1024)}, u32[]{:S(2)}) copy-start(f32[1280]{0:T(1024)} %param.19) | copy-start | bytes 15364
  1.0 6.9 %collective-permute-start = (bf16[2,16,2560]{2,1,0:T(8,128)(2,1)S(1)}, bf16[2,16,2560]{2,1,0:T(8,128)(2,1)S(1)}, u32[]{:S(2)}, u32[]{:S(2)}) collective-permute-start(bf16[2,16,2560]{2,1,0:T(8,128)(2,1)S(1)} %slice.16), channel_id=1, source_target_pairs={{0,4},{4,8},{8,12},{12,16},{16,20},{20,24},{24,28},{1,5},{5,9},{9,... | collective-permute-start | bytes 491528 | tf_op jit(solution)/shard_map/ppermute | solution.py:25
  2.5 31.0 %copy-start.4 = (bf16[40,1280]{1,0:T(8,128)(2,1)}, bf16[40,1280]{1,0:T(8,128)(2,1)S(1)}, u32[]{:S(2)}) copy-start(bf16[40,1280]{1,0:T(8,128)(2,1)S(1)} %fusion.3.expand_ref) | copy-start | bytes 307204
  8.2 25.2 %copy-start.7 = (f32[4,1280]{1,0:T(4,128)S(1)}, f32[4,1280]{1,0:T(4,128)}, u32[]{:S(2)}) copy-start(f32[4,1280]{1,0:T(4,128)} %kernel_ref.1) | copy-start | bytes 61444
  8.2 25.2 %copy-start.8 = (f32[4,256]{1,0:T(4,128)S(1)}, f32[4,256]{1,0:T(4,128)}, u32[]{:S(2)}) copy-start(f32[4,256]{1,0:T(4,128)} %bc_kernel_ref.1) | copy-start | bytes 12292
  8.2 25.2 %copy-start.9 = (f32[20]{0:T(128)S(1)}, f32[20]{0:T(128)}, u32[]{:S(2)}) copy-start(f32[20]{0:T(128)} %param.17) | copy-start | bytes 244
  8.2 25.2 %copy-start.10 = (f32[20]{0:T(128)S(1)}, f32[20]{0:T(128)}, u32[]{:S(2)}) copy-start(f32[20]{0:T(128)} %param.18) | copy-start | bytes 244
  31.9 1.5 %copy-start.6 = (bf16[2,528,1280]{2,1,0:T(8,128)(2,1)}, bf16[2,528,1280]{2,1,0:T(8,128)(2,1)S(1)}, u32[]{:S(2)}) copy-start(bf16[2,528,1280]{2,1,0:T(8,128)(2,1)S(1)} %get-tuple-element.15.pre_ref) | copy-start | bytes 8110084
  50.2 1.5 %copy-start = (bf16[2,512,1280]{2,1,0:T(8,128)(2,1)}, bf16[2,512,1280]{2,1,0:T(8,128)(2,1)S(1)}, u32[]{:S(2)}) copy-start(bf16[2,512,1280]{2,1,0:T(8,128)(2,1)S(1)} %get-tuple-element.17.scaled_ref) | copy-start | bytes 7864324
  51.7 0.8 copy-start.1
  52.6 0.8 copy-start.2
  53.4 0.8 copy-start.3
  54.2 0.6 copy-start.5
